TPU v7x, 512 devices: a whole 4x4x16 slice. The times are simulated.
512 devices in a mesh: seq: 128 (over z, y, core), rep: 4 (over x).
Axes of the slice: x: 4, y: 4, z: 16, core: 2. Of those that a mesh axis runs over, the one named last changes fastest.
Arguments:
- queries: bfloat16 [512, 32, 128], P('seq', 'rep'), may hold values from -48 to 48
- key_cache: bfloat16 [8, 262144, 128], P('rep', 'seq'), may hold values from -6 to 6
- value_cache: bfloat16 [8, 262144, 128], P('rep', 'seq'), may hold values from -6 to 6
- summary_keys: bfloat16 [8, 128, 128], P('rep', 'seq'), may hold values from -16 to 16
- summary_values: bfloat16 [8, 128, 128], P('rep', 'seq'), may hold values from -6 to 6
- owner_map: int32 [128], replicated, may hold values from 0 to 127, each once
- super_ids: int32 [512, 8, 4], P(None, 'rep'), may hold values from 0 to 127, as said below
- fine_ids: int32 [512, 8, 16], P(None, 'rep'), may hold values from 0 to 63, all different within a row
Outputs:
- attended: bfloat16 [512, 32, 128], P(('seq', 'rep'))
Inputs may be any that keep to these rules, and one draw needn't show every extreme that they name: `super_ids`: each row names 4 different super-blocks; among the rows of one sender group (the 4 requests of one index of seq with the 2 key-value heads of one index of rep) no super-block is named more than 2 times, and in every such group some super-block is named exactly 2 times. `fine_ids`: each row names 16 different positions; position p is block p % 16 of super-block super_ids[r, g, p // 16]. `owner_map`: a permutation; slot q covers fine blocks q * 16 to q * 16 + 15 of the caches.
All inputs are finite; a program needn't handle non-finite values.
Results may differ from a plain program's by a relative error of at most 0.004.
Values may be sent and summed in bfloat16 or wider, within the bound.
A program may use at most 64 MiB of HBM per device.

v0:
```python
import math

import jax
import jax.numpy as jnp
from jax import lax
from jax.sharding import PartitionSpec as P

SUPER = 16


NEGATIVE = -1e30


def in_one_piece(arrays, axis, dim, along):
    ends, at = ([], 0)
    for a in arrays[:-1]:
        at += a.shape[along]
        ends.append(at)
    both = jnp.concatenate(arrays, axis=along)
    return tuple(jnp.split(lax.all_gather(both, axis, axis=dim, tiled=True), ends, axis=along))


def combine(earlier, later):
    highest = jnp.maximum(earlier[0], later[0])
    left_factor = jnp.exp(earlier[0] - highest)
    right_factor = jnp.exp(later[0] - highest)
    return (
        highest,
        earlier[1] * left_factor + later[1] * right_factor,
        earlier[2] * left_factor[..., None] + later[2] * right_factor[..., None],
    )


def coarse_terms(query_rows, summary_keys, summary_values, kept_slots):
    scaling = query_rows.shape[-1] ** (-0.5)
    scores = jnp.einsum(
        "bgqd,gsd->bgqs", query_rows, summary_keys, preferred_element_type=jnp.float32
    ) * scaling + math.log(SUPER)
    scores = jnp.where(kept_slots[:, :, None, :], scores, NEGATIVE)
    highest = jnp.max(scores, axis=3)
    weights = jnp.where(kept_slots[:, :, None, :], jnp.exp(scores - highest[..., None]), 0.0)
    weighted = jnp.einsum("bgqs,gsd->bgqd", weights, summary_values.astype(jnp.float32))
    return (highest, jnp.sum(weights, axis=3), weighted)


def gathered_coarse(queries, summary_keys, summary_values, own_slots, slot_count):
    own_rows, heads, head_dim = queries.shape
    groups = summary_keys.shape[0]
    every_key, every_value = in_one_piece((summary_keys, summary_values), "seq", 1, 0)
    kept_all = jnp.logical_not(
        jnp.any(own_slots[..., None] == jnp.arange(slot_count, dtype=jnp.int32), axis=2)
    )
    own_queries = queries.reshape(own_rows, groups, heads // groups, head_dim)
    return coarse_terms(own_queries, every_key, every_value, kept_all)


def holder_block(query_rows, meta_rows, keys_here, values_here):
    row_total, per_group, head_dim = query_rows.shape
    groups, span, unused = keys_here.shape
    scaling = head_dim ** (-0.5)
    row_step = math.gcd(row_total, 64)
    wide_values = values_here.astype(jnp.float32)

    def one_block(pieces):
        query_block, meta_block = pieces
        scores = (
            jnp.einsum("rqd,gtd->rgqt", query_block, keys_here, preferred_element_type=jnp.float32)
            * scaling
        )
        head_ok = meta_block[:, SUPER][:, None] == jnp.arange(groups, dtype=jnp.int32)[None, :]
        block_ok = meta_block[:, :SUPER] > 0
        allowed = jnp.logical_and(head_ok[:, :, None], block_ok[:, None, :])
        shaped = scores.reshape(row_step, groups, per_group, SUPER, span // SUPER)
        token_mask = allowed[:, :, None, :, None]
        shaped = jnp.where(token_mask, shaped, NEGATIVE)
        highest = jnp.max(shaped, axis=(1, 3, 4))
        weights = jnp.where(token_mask, jnp.exp(shaped - highest[:, None, :, None, None]), 0.0)
        weight_sum = jnp.sum(weights, axis=(1, 3, 4))
        weighted = jnp.einsum(
            "rgqt,gtd->rqd", weights.reshape(row_step, groups, per_group, span), wide_values
        )
        return (highest, weight_sum, weighted)

    blocks = (
        query_rows.reshape(row_total // row_step, row_step, per_group, head_dim),
        meta_rows.reshape(row_total // row_step, row_step, meta_rows.shape[1]),
    )
    highest, weight_sum, weighted = lax.map(one_block, blocks)
    return (
        highest.reshape(row_total, per_group),
        weight_sum.reshape(row_total, per_group),
        weighted.reshape(row_total, per_group, head_dim),
    )


def routed_fine(queries, key_cache, value_cache, own_slots, own_fine, supers_here, slot_count):
    own_rows, heads, head_dim = queries.shape
    groups = key_cache.shape[0]
    per_group = heads // groups
    chosen_count = own_slots.shape[2]
    capacity = max(2, (own_rows * groups * chosen_count + slot_count - 2) // (slot_count - 1))
    items = own_rows * groups * chosen_count
    item_slot = own_slots.reshape(items)
    order = jnp.arange(items, dtype=jnp.int32)
    earlier_same = jnp.logical_and(
        item_slot[:, None] == item_slot[None, :], order[None, :] < order[:, None]
    )
    rank = jnp.sum(earlier_same.astype(jnp.int32), axis=1)
    bucket = item_slot * capacity + rank
    total = slot_count * capacity
    place = bucket[:, None] == jnp.arange(total, dtype=jnp.int32)[None, :]
    query_rows = queries.reshape(own_rows * groups, per_group * head_dim)
    item_queries = jnp.repeat(query_rows, chosen_count, axis=0)
    sent_queries = jnp.dot(
        place.T.astype(jnp.bfloat16), item_queries, preferred_element_type=jnp.float32
    )
    sent_queries = sent_queries.astype(jnp.bfloat16).reshape(
        slot_count, capacity, per_group * head_dim
    )
    positions = (
        jnp.arange(chosen_count, dtype=jnp.int32)[:, None] * SUPER
        + jnp.arange(SUPER, dtype=jnp.int32)[None, :]
    )
    picked_bits = jnp.any(
        own_fine[:, :, None, None, :] == positions[None, None, :, :, None], axis=4
    ).astype(jnp.int32)
    item_group = jnp.broadcast_to(
        jnp.arange(groups, dtype=jnp.int32)[None, :, None], (own_rows, groups, chosen_count)
    )
    item_meta = jnp.concatenate(
        [picked_bits.reshape(items, SUPER), item_group.reshape(items, 1)], axis=1
    )
    sent_meta = jnp.sum(jnp.where(place[:, :, None], item_meta[:, None, :], 0), axis=0)
    sent_meta = sent_meta.reshape(slot_count, capacity, SUPER + 1)
    got_queries = lax.all_to_all(sent_queries, "seq", split_axis=0, concat_axis=0, tiled=True)
    got_meta = lax.all_to_all(sent_meta, "seq", split_axis=0, concat_axis=0, tiled=True)
    count = got_queries.shape[1]
    seq_count = got_queries.shape[0] // supers_here
    shaped_queries = got_queries.reshape(seq_count, supers_here, count, per_group, head_dim)
    shaped_meta = got_meta.reshape(seq_count, supers_here, count, SUPER + 1)
    highest, weight_sum, weighted = holder_block(
        shaped_queries[:, 0].reshape(seq_count * count, per_group, head_dim),
        shaped_meta[:, 0].reshape(seq_count * count, SUPER + 1),
        key_cache,
        value_cache,
    )
    peaks = [highest.reshape(seq_count, count, per_group)]
    sums = [weight_sum.reshape(seq_count, count, per_group)]
    weighted_parts = [weighted.reshape(seq_count, count, per_group, head_dim)]
    peak_all = jnp.stack(peaks, axis=1).reshape(seq_count * supers_here, count, per_group)
    sum_all = jnp.stack(sums, axis=1).reshape(seq_count * supers_here, count, per_group)
    weighted_all = jnp.stack(weighted_parts, axis=1).reshape(
        seq_count * supers_here, count, per_group, head_dim
    )
    back_peak = lax.all_to_all(peak_all, "seq", split_axis=0, concat_axis=0, tiled=True)
    back_sum = lax.all_to_all(sum_all, "seq", split_axis=0, concat_axis=0, tiled=True)
    back_weighted = lax.all_to_all(weighted_all, "seq", split_axis=0, concat_axis=0, tiled=True)
    item_peak = jnp.take(back_peak.reshape(total, per_group), bucket, axis=0)
    item_sum = jnp.take(back_sum.reshape(total, per_group), bucket, axis=0)
    item_weighted = jnp.take(back_weighted.reshape(total, per_group, head_dim), bucket, axis=0)
    item_peak = item_peak.reshape(own_rows, groups, chosen_count, per_group)
    item_sum = item_sum.reshape(own_rows, groups, chosen_count, per_group)
    item_weighted = item_weighted.reshape(own_rows, groups, chosen_count, per_group, head_dim)
    peak = jnp.max(item_peak, axis=2)
    factor = jnp.exp(item_peak - peak[:, :, None, :])
    return (
        peak,
        jnp.sum(item_sum * factor, axis=2),
        jnp.sum(item_weighted * factor[..., None], axis=2),
    )


def shards(
    queries, key_cache, value_cache, summary_keys, summary_values, owner_map, super_ids, fine_ids
):
    groups = key_cache.shape[0]
    head_dim = queries.shape[2]
    per_group = queries.shape[1] // groups
    supers_here = summary_keys.shape[1]
    slot_count = owner_map.shape[0]
    my_index = lax.axis_index("seq")
    own_rows = queries.shape[0]
    is_super = super_ids[..., None] == jnp.arange(slot_count, dtype=jnp.int32)
    slots = jnp.sum(jnp.where(is_super, owner_map, 0), axis=3)
    own_slots = lax.dynamic_slice_in_dim(slots, my_index * own_rows, own_rows, 0)
    own_fine = lax.dynamic_slice_in_dim(fine_ids, my_index * own_rows, own_rows, 0)
    merged = routed_fine(
        queries, key_cache, value_cache, own_slots, own_fine, supers_here, slot_count
    )
    merged = combine(
        merged, gathered_coarse(queries, summary_keys, summary_values, own_slots, slot_count)
    )
    result = (
        (merged[2] / merged[1][..., None])
        .reshape(own_rows, groups * per_group, head_dim)
        .astype(jnp.bfloat16)
    )
    return lax.all_to_all(result, "rep", split_axis=0, concat_axis=1, tiled=True)


def solution(mesh):
    in_specs = (
        P("seq", "rep", None),
        P("rep", "seq", None),
        P("rep", "seq", None),
        P("rep", "seq", None),
        P("rep", "seq", None),
        P(),
        P(None, "rep", None),
        P(None, "rep", None),
    )
    out_specs = P(("seq", "rep"), None, None)
    return jax.shard_map(shards, mesh=mesh, in_specs=in_specs, out_specs=out_specs, check_vma=False)
```

profile of v0, /device:TPU:1, one launch (start us, length us, event | category | flops | bytes accessed | tf_op | source)
XLA Modules:
  0.0 261.4 jit_solution(11125759675261475811)
XLA Ops:
  0.0 2.0 select_reduce_fusion
  2.3 0.2 convert_reduce_fusion
  2.8 0.7 compare_reduce_fusion
  3.8 0.2 select_reduce_fusion.1
  4.0 0.8 copy.173
  4.7 20.6 %all-to-all-start = ((s32[128,2,17]{2,1,0:T(2,128)}), s32[128,2,17]{2,1,0:T(2,128)S(1)}, u32[]{:S(2)}, u32[]{:S(2)}) async-start(s32[128,2,17]{2,1,0:T(2,128)} %bitcast.14), calls=%async_computation | async-start | bytes 262144 | tf_op jit(solution)/shard_map/all_to_all | solution.py:136
  25.3 0.7 reshape.217
  26.1 0.3 convolution_convert_fusion
  26.4 0.8 reshape.219
  27.2 14.1 %all-to-all-done = s32[128,2,17]{2,1,0:T(2,128)S(1)} async-done(((s32[128,2,17]{2,1,0:T(2,128)}), s32[128,2,17]{2,1,0:T(2,128)S(1)}, u32[]{:S(2)}, u32[]{:S(2)}) %all-to-all-start) | async-done | bytes 17440 | tf_op jit(solution)/shard_map/all_to_all | solution.py:136
  41.3 7.2 %all-to-all-start.1 = ((bf16[128,2,512]{2,1,0:T(2,128)(2,1)}), bf16[128,2,512]{2,1,0:T(2,128)(2,1)S(1)}, u32[]{:S(2)}, u32[]{:S(2)}) async-start(bf16[128,2,512]{2,1,0:T(2,128)(2,1)} %reshape.219), calls=%async_computation.1 | async-start | bytes 524288 | tf_op jit(solution)/shard_map/all_to_all | solution.py:135
  48.6 20.3 %all-to-all-done.1 = bf16[128,2,512]{2,1,0:T(2,128)(2,1)S(1)} async-done(((bf16[128,2,512]{2,1,0:T(2,128)(2,1)}), bf16[128,2,512]{2,1,0:T(2,128)(2,1)S(1)}, u32[]{:S(2)}, u32[]{:S(2)}) %all-to-all-start.1) | async-done | bytes 262176 | tf_op jit(solution)/shard_map/all_to_all | solution.py:135
  69.0 0.2 reshape_reshape_squeeze_reshape.7
  69.2 24.1 %while.14 = (s32[]{:T(128)}, f32[4,64,4]{1,2,0:T(4,128)S(1)}, f32[4,64,4]{1,2,0:T(4,128)S(1)}, f32[4,64,4,128]{3,1,0,2:T(8,128)S(1)}, s32[4,64,17]{1,2,0:T(8,128...) while((s32[]{:T(128)}, f32[4,64,4]{1,2,0:T(4,128)S(1)}, ...), condition=%wide.region_7.8_spmd, body=%wide.region_4.7_spmd.sunk | while | flops 549456512 | bytes 21072520 | solution.py:88
  69.2 0.1 copy.235
  69.4 0.3 broadcast_in_dim.242
  69.8 0.3 broadcast_in_dim.243
  70.1 2.2 bitcast_reduce_fusion.2
  72.3 1.6 fusion.57
  73.9 1.3 fusion.56
  75.2 0.1 copy.235
  75.4 0.3 broadcast_in_dim.242
  75.8 0.3 broadcast_in_dim.243
  76.1 2.2 bitcast_reduce_fusion.2
  78.3 1.6 fusion.57
  80.0 1.3 fusion.56
  81.3 0.1 copy.235
  81.5 0.3 broadcast_in_dim.242
  81.8 0.3 broadcast_in_dim.243
  82.1 2.2 bitcast_reduce_fusion.2
  84.3 1.6 fusion.57
  86.0 1.3 fusion.56
  87.3 0.1 copy.235
  87.5 0.3 broadcast_in_dim.242
  87.8 0.3 broadcast_in_dim.243
  88.2 2.2 bitcast_reduce_fusion.2
  90.4 1.6 fusion.57
  92.0 1.3 fusion.56
  93.3 0.8 copy.180
  94.1 8.3 %all-to-all-start.3 = ((f32[128,2,4]{2,1,0:T(2,128)}), f32[128,2,4]{2,1,0:T(2,128)S(1)}, u32[]{:S(2)}, u32[]{:S(2)}) async-start(f32[128,2,4]{2,1,0:T(2,128)} %bitcast.21), calls=%async_computation.3 | async-start | bytes 262144 | tf_op jit(solution)/shard_map/all_to_all | solution.py:155
  102.5 0.8 copy.191
  103.3 15.0 %all-to-all-done.3 = f32[128,2,4]{2,1,0:T(2,128)S(1)} async-done(((f32[128,2,4]{2,1,0:T(2,128)}), f32[128,2,4]{2,1,0:T(2,128)S(1)}, u32[]{:S(2)}, u32[]{:S(2)}) %all-to-all-start.3) | async-done | bytes 4128 | tf_op jit(solution)/shard_map/all_to_all | solution.py:155
  118.4 7.4 %all-to-all-start.4 = ((f32[128,2,4]{2,1,0:T(2,128)}), f32[128,2,4]{2,1,0:T(2,128)S(1)}, u32[]{:S(2)}, u32[]{:S(2)}) async-start(f32[128,2,4]{2,1,0:T(2,128)} %bitcast.31), calls=%async_computation.4 | async-start | bytes 262144 | tf_op jit(solution)/shard_map/all_to_all | solution.py:156
  125.8 1.0 copy.177
  126.7 15.0 %all-to-all-done.4 = f32[128,2,4]{2,1,0:T(2,128)S(1)} async-done(((f32[128,2,4]{2,1,0:T(2,128)}), f32[128,2,4]{2,1,0:T(2,128)S(1)}, u32[]{:S(2)}, u32[]{:S(2)}) %all-to-all-start.4) | async-done | bytes 4128 | tf_op jit(solution)/shard_map/all_to_all | solution.py:156
  141.8 7.2 %all-to-all-start.2 = ((f32[128,2,4,128]{3,1,2,0:T(2,128)}), f32[128,2,4,128]{3,1,2,0:T(2,128)S(1)}, u32[]{:S(2)}, u32[]{:S(2)}) async-start(f32[128,2,4,128]{3,1,2,0:T(2,128)} %copy.177), calls=%async_computation.2 | async-start | bytes 1048576 | tf_op jit(solution)/shard_map/all_to_all | solution.py:157
  149.3 0.1 copy.169
  149.4 99.6 %all_gather.3 = bf16[4,128,128]{2,0,1:T(4,128)(2,1)S(1)} all-gather(bf16[4,1,128]{2,0,1:T(4,128)(2,1)S(1)} %pad_maximum_fusion), channel_id=1, replica_groups=mesh['seq'=128,'rep'=4] {'seq'}, dimensions={1}, use_global_device_ids=true | all-gather | bytes 132096 | tf_op jit(solution)/shard_map/all_gather | solution.py:20
  249.2 0.2 fusion.48
  249.4 0.2 fusion.36
  249.6 0.6 gather_fusion.1
  250.2 0.6 gather_fusion.2
  250.8 0.1 copy.199
  251.0 0.1 copy.200
  251.1 0.1 copy.204
  251.2 0.2 multiply_reduce_fusion.1
  251.4 0.1 copy.193
  251.5 0.1 copy.182
  251.7 0.1 copy.178
  251.9 0.6 gather_fusion
  252.5 0.1 multiply_reduce_fusion
  252.6 0.2 fusion.33
  252.8 8.0 %all_to_all.37 = bf16[4,8,128]{2,1,0:T(8,128)(2,1)S(1)} all-to-all(bf16[4,8,128]{2,1,0:T(8,128)(2,1)S(1)} %bitcast.132), channel_id=1, replica_groups=mesh['seq'=128,'rep'=4] {'rep'}, dimensions={0} | all-to-all | bytes 16384 | tf_op jit(solution)/shard_map/all_to_all | solution.py:198
  260.8 0.6 copy.254
  (83 shorter events, 2.4 us)
Async XLA Ops:
  0.0 2.6 copy-start
  4.7 36.6 %all-to-all-start = ((s32[128,2,17]{2,1,0:T(2,128)}), s32[128,2,17]{2,1,0:T(2,128)S(1)}, u32[]{:S(2)}, u32[]{:S(2)}) async-start(s32[128,2,17]{2,1,0:T(2,128)} %bitcast.14), calls=%async_computation | async-start | bytes 262144 | tf_op jit(solution)/shard_map/all_to_all | solution.py:136
  41.3 27.7 %all-to-all-start.1 = ((bf16[128,2,512]{2,1,0:T(2,128)(2,1)}), bf16[128,2,512]{2,1,0:T(2,128)(2,1)S(1)}, u32[]{:S(2)}, u32[]{:S(2)}) async-start(bf16[128,2,512]{2,1,0:T(2,128)(2,1)} %reshape.219), calls=%async_computation.1 | async-start | bytes 524288 | tf_op jit(solution)/shard_map/all_to_all | solution.py:135
  69.1 80.3 %copy-start.2 = (bf16[2,1,128]{2,0,1:T(2,128)(2,1)S(1)}, bf16[2,1,128]{2,0,1:T(2,128)(2,1)}, u32[]{:S(2)}) copy-start(bf16[2,1,128]{2,0,1:T(2,128)(2,1)} %param.16) | copy-start | bytes 1540
  69.1 80.2 %copy-start.3 = (bf16[2,1,128]{2,0,1:T(2,128)(2,1)S(1)}, bf16[2,1,128]{2,0,1:T(2,128)(2,1)}, u32[]{:S(2)}) copy-start(bf16[2,1,128]{2,0,1:T(2,128)(2,1)} %param.15) | copy-start | bytes 1540
  69.2 180.0 %copy-start.1 = (bf16[4,8,128]{2,1,0:T(8,128)(2,1)S(1)}, bf16[4,8,128]{2,1,0:T(8,128)(2,1)}, u32[]{:S(2)}) copy-start(bf16[4,8,128]{2,1,0:T(8,128)(2,1)} %param.12) | copy-start | bytes 24580
  69.8 2.5 copy-start.4
  75.8 2.5 copy-start.4
  81.8 2.5 copy-start.4
  87.8 2.5 copy-start.4
  94.1 24.3 %all-to-all-start.3 = ((f32[128,2,4]{2,1,0:T(2,128)}), f32[128,2,4]{2,1,0:T(2,128)S(1)}, u32[]{:S(2)}, u32[]{:S(2)}) async-start(f32[128,2,4]{2,1,0:T(2,128)} %bitcast.21), calls=%async_computation.3 | async-start | bytes 262144 | tf_op jit(solution)/shard_map/all_to_all | solution.py:155
  118.4 23.4 %all-to-all-start.4 = ((f32[128,2,4]{2,1,0:T(2,128)}), f32[128,2,4]{2,1,0:T(2,128)S(1)}, u32[]{:S(2)}, u32[]{:S(2)}) async-start(f32[128,2,4]{2,1,0:T(2,128)} %bitcast.31), calls=%async_computation.4 | async-start | bytes 262144 | tf_op jit(solution)/shard_map/all_to_all | solution.py:156
  141.8 109.9 %all-to-all-start.2 = ((f32[128,2,4,128]{3,1,2,0:T(2,128)}), f32[128,2,4,128]{3,1,2,0:T(2,128)S(1)}, u32[]{:S(2)}, u32[]{:S(2)}) async-start(f32[128,2,4,128]{3,1,2,0:T(2,128)} %copy.177), calls=%async_computation.2 | async-start | bytes 1048576 | tf_op jit(solution)/shard_map/all_to_all | solution.py:157
where the time goes:
time: 262 us; the launch traced here: 261 us
  blocking collectives  108 us (41%)
  waiting for transfers between devices  64.5 us (25%)
  starting transfers between devices  50.6 us (19%)
  matrix products  16 us (6%)
  local copies, waits for them, and re-layouts  12.5 us (5%)
  other arithmetic  9.66 us (4%)
    all_gather x1, blocking collectives, in_one_piece(): lax.all_gather(both, axis, axis=dim, tiled=True)  99.6 us
    all_to_all x1, starting transfers between devices, routed_fine(): lax.all_to_all(sent_meta, 'seq', split_axis=0, concat_axis=0, tiled=True)  20.6 us
    all_to_all x1, waiting for transfers between devices, routed_fine(): lax.all_to_all(sent_queries, 'seq', split_axis=0, concat_axis=0, tiled=True)  20.3 us
    all_to_all x1, waiting for transfers between devices, routed_fine(): lax.all_to_all(sum_all, 'seq', split_axis=0, concat_axis=0, tiled=True)  15 us
    all_to_all x1, waiting for transfers between devices, routed_fine(): lax.all_to_all(peak_all, 'seq', split_axis=0, concat_axis=0, tiled=True)  15 us
    all_to_all x1, waiting for transfers between devices, routed_fine(): lax.all_to_all(sent_meta, 'seq', split_axis=0, concat_axis=0, tiled=True)  14.1 us
    dot_general x4, matrix products, one_block(): jnp.einsum('rqd,gtd->rgqt', query_block, keys_here, preferred_element_typ...  8.72 us
    all_to_all x1, starting transfers between devices, routed_fine(): lax.all_to_all(peak_all, 'seq', split_axis=0, concat_axis=0, tiled=True)  8.3 us
  transfers between devices with their start and end apart: 5, of which 4 were waited for; matrix products, arithmetic and copies ran while one was open for 3% of the time, Pallas kernels for 0%

commit v1 on v0

v1 whole, which is shorter than its diff:
```python
import functools
import math

import jax
import jax.numpy as jnp
from jax import lax
from jax.experimental import pallas as pl
from jax.experimental.pallas import tpu as pltpu
from jax.sharding import PartitionSpec as P

MESH = pl.DeviceIdType.MESH
F32, BF16, I32 = jnp.float32, jnp.bfloat16, jnp.int32
NZ, NP, NY, NX = 16, 8, 4, 4
HD, BLK, SUPER, NSEL, NFINE = 128, 128, 16, 4, 16
NREQ, SPAN = 512, 2048
NEG = -1e30
SCALE2 = HD**-0.5 / math.log(2.0)
Z_ORDER = (8, 7, 9, 6, 10, 5, 11, 4, 12, 3, 13, 2, 14, 1, 15)


def iota(shape, dim):
    return lax.broadcasted_iota(I32, shape, dim)


def dot(a, b, dims=((1,), (0,))):
    return lax.dot_general(a, b, (dims, ((), ())), preferred_element_type=F32)


def group_rank(hits):
    i = jnp.bitwise_and(iota(hits[0].shape, 1), 3)
    before, total = [], []
    for h in hits:
        b = jnp.zeros_like(h)
        t = h
        for d in (1, 2, 3):
            b = b + jnp.where(i >= d, pltpu.roll(h, d, 1), 0)
            t = t + jnp.where(i + d <= 3, pltpu.roll(h, NREQ - d, 1), 0)
        before.append(b)
        total.append(t + b)
    return before[0], before[1] + total[0]


def kernel(
    q_h, kc_h, vc_h, sk_h, sv_h, om_h, si_h, fi_h, o_ref,
    sk, sv, om, si, fi, kcat, vcat, v_t, qz, qs, rq, rsel, meta, s_s, p_s,
    os_, ol, ro, rl, pzs, lzs, pz, lz, sz, szf, sf, xs,
    load_sem, kv_sem, q1s, q1r, q2s, q2r, r1s, r1r, l1s, l1r, r2s, r2r, l2s, l2r, szs, szr, sfs, sfr, xss, xsr, loc,
):
    me, rep = lax.axis_index("seq"), lax.axis_index("rep")
    z, p = me // NP, lax.rem(me, NP)
    y, c = p // 2, lax.rem(p, 2)

    def z_peer(d):
        return lax.rem(z + d, NZ)

    def plane_peer(dy, dc):
        return lax.rem(y + dy, NY) * 2 + lax.rem(c + dc, 2)

    plane = [(dy, dc) for dy in (2, 1, 3, 0) for dc in (0, 1) if dy or dc]

    barrier = pltpu.get_barrier_semaphore()
    for d in Z_ORDER:
        pl.semaphore_signal(barrier, inc=1, device_id=(z_peer(d) * NP + p, rep), device_id_type=MESH)
    for dy, dc in plane:
        pl.semaphore_signal(barrier, inc=1, device_id=(z * NP + plane_peer(dy, dc), rep), device_id_type=MESH)
    for d in range(1, NX):
        pl.semaphore_signal(barrier, inc=1, device_id=(me, lax.rem(rep + d, NX)), device_id_type=MESH)

    def remote(src, dst, ss, rs, seq, x=None):
        return pltpu.make_async_remote_copy(
            src_ref=src, dst_ref=dst, send_sem=ss, recv_sem=rs,
            device_id=(seq, rep if x is None else x), device_id_type=MESH,
        )

    def wait(ref, sem):
        pltpu.make_async_copy(ref, ref, sem).wait()

    loads = [
        pltpu.make_async_copy(a, b, load_sem.at[n])
        for n, (a, b) in enumerate([(q_h, qz.at[z]), (sk_h, sk), (sv_h, sv), (om_h, om), (si_h, si), (fi_h, fi)])
    ]
    kv_loads = [
        pltpu.make_async_copy(a.at[g], b.at[:, pl.ds(g * HD, HD)], kv_sem.at[2 * n + g])
        for n, (a, b) in enumerate([(kc_h, kcat), (vc_h, vcat)])
        for g in (0, 1)
    ]
    for copy in loads + kv_loads:
        copy.start()
    for copy in loads:
        copy.wait()
    sz[z] = jnp.concatenate([sk[...].astype(F32), sv[...].astype(F32)], axis=0).astype(BF16)

    pl.semaphore_wait(barrier, len(Z_ORDER) + len(plane) + NX - 1)

    for d in Z_ORDER:
        remote(qz.at[z], qz.at[z], q1s, q1r, z_peer(d) * NP + p).start()
    for d in Z_ORDER:
        remote(sz.at[z], sz.at[z], szs, szr, z_peer(d) * NP + p).start()

    omv = om[...]
    siv = [[si[g, j : j + 1, :] for j in range(NSEL)] for g in (0, 1)]
    lane128 = iota((NP, 128), 1)
    sig8 = jnp.sum(jnp.where(omv == z * NP + iota((NP, 128), 0), lane128, 0), axis=1, keepdims=True)
    hits = []
    for g in (0, 1):
        h = siv[g][0] == sig8
        for j in range(1, NSEL):
            h = jnp.logical_or(h, siv[g][j] == sig8)
        hits.append(jnp.where(h, 1, 0))
    ranks = group_rank(hits)
    row, lane = iota((NREQ, NREQ), 0), iota((NREQ, NREQ), 1)
    source = (lane >> 5) * 32 + p * 4 + ((lane >> 3) & 3)
    picked = jnp.zeros((NP, NREQ), F32)
    for g in (0, 1):
        spread = jnp.where(row == jnp.where(((lane >> 2) & 1) == g, source, -1), 1.0, 0.0).astype(BF16)
        code = jnp.where(hits[g] > 0, ranks[g] + 1, 0).astype(F32).astype(BF16)
        picked = picked + dot(code, spread)
    rsel[...] = picked

    sig1 = jnp.sum(jnp.where(omv == me, lane128[0:1], 0), axis=1, keepdims=True)
    own_hits, own_bits = [], []
    for g in (0, 1):
        h, jsel = jnp.zeros((1, NREQ), I32), jnp.zeros((1, NREQ), I32)
        for j in range(NSEL):
            same = siv[g][j] == sig1
            h = jnp.where(same, 1, h)
            jsel = jnp.where(same, j, jsel)
        target = jsel * SUPER + iota((SUPER, NREQ), 0)
        bits = fi[g, 0:1, :] == target
        for k in range(1, NFINE):
            bits = jnp.logical_or(bits, fi[g, k : k + 1, :] == target)
        own_hits.append(jnp.broadcast_to(h, (8, NREQ)))
        own_bits.append(jnp.where(bits, 1.0, 0.0))
    own_ranks = group_rank(own_hits)
    sub8 = iota((8, NREQ), 0)
    stacked = []
    for slot in (0, 1):
        use = [jnp.where(jnp.logical_and(own_hits[g] > 0, own_ranks[g] == slot), 1.0, 0.0) for g in (0, 1)]
        wanted = own_bits[0] * use[0][0:1] + own_bits[1] * use[1][0:1]
        flags = jnp.where(sub8 == 0, use[0], jnp.where(sub8 == 1, use[1], 0.0))
        stacked.append(jnp.concatenate([wanted, flags, jnp.zeros((8, NREQ), F32)], axis=0).astype(BF16))
    for chunk in range(NY):
        row, col = iota((NREQ, 256), 0), iota((NREQ, 256), 1)
        sender = ((col >> 3) & 15) * NP + chunk * 2 + (col >> 7)
        acc = jnp.zeros((32, 256), F32)
        for slot in (0, 1):
            at = jnp.where(((col >> 2) & 1) == slot, sender, -1)
            acc = acc + dot(stacked[slot], jnp.where((row >> 2) == at, 1.0, 0.0).astype(BF16))
        meta[chunk] = acc

    srow, slane = iota((128, NREQ), 0), iota((128, NREQ), 1)
    base = jnp.where(
        jnp.logical_and((srow >> 3) == (slane >> 5), (srow & 3) == (slane & 3)), ((srow >> 2) & 1) + 1, -1
    ).astype(F32)

    wait(qz.at[pl.ds(0, NZ - 1)], q1r)
    every = qz[...].reshape(NREQ, HD)
    for dy, dc in [(0, 0)] + plane:
        peer = plane_peer(dy, dc)
        choose = jnp.where(base == rsel[pl.ds(peer, 1), :], 1.0, 0.0).astype(BF16)
        qs[peer] = dot(choose, every).astype(BF16)
        if dy or dc:
            remote(qs.at[peer], rq.at[p], q2s, q2r.at[dy], z * NP + peer).start()
        else:
            pltpu.make_async_copy(qs.at[peer], rq.at[peer], loc.at[0]).start()

    wait(sz.at[pl.ds(0, NZ - 1)], szr)
    for n in range(NZ):
        szf[n * 4 : n * 4 + 4, :] = sz[n].astype(F32)
    sf[p] = szf[...].astype(BF16)
    for dy, dc in plane:
        remote(sf.at[p], sf.at[p], sfs, sfr, z * NP + plane_peer(dy, dc)).start()

    for copy in kv_loads:
        copy.wait()
    v_t[...] = jnp.transpose(vcat[...], (1, 0))
    wait(qs.at[0], loc.at[0])

    def chunk_step(k, carry):
        @pl.when(k == 0)
        def _():
            wait(rq.at[0], q2r.at[0])

        @pl.when(k > 0)
        def _():
            wait(rq.at[pl.ds(0, 2)], q2r.at[k])

        yy = lax.rem(y + NY - k, NY)
        m_all = meta[yy]
        flags = jnp.transpose(m_all[16:24], (1, 0)).astype(BF16)
        rows = rq[pl.ds(yy * 2, 2)].reshape(256, HD)
        split = jnp.concatenate([rows * flags[:, 0:1], rows * flags[:, 1:2]], axis=1)
        s_s[...] = dot(kcat[...], split, ((1,), (1,)))
        bias = jnp.where(m_all[0:16] > 0.5, 0.0, NEG)
        peak = jnp.full((1, 256), -3e38, F32)
        for b in range(SUPER):
            top = jnp.max(s_s[b * BLK : (b + 1) * BLK, :], axis=0, keepdims=True)
            peak = jnp.maximum(peak, top + bias[b : b + 1])
        total = jnp.zeros((1, 256), F32)
        for b in range(SUPER):
            w = jnp.exp2((s_s[b * BLK : (b + 1) * BLK, :] + (bias[b : b + 1] - peak)) * SCALE2)
            total = total + jnp.sum(w, axis=0, keepdims=True)
            p_s[b * BLK : (b + 1) * BLK, :] = w.astype(BF16)
        out = dot(v_t[...], p_s[...])
        out = jnp.where(m_all[17:18] > 0.5, out[HD : 2 * HD], out[0:HD]) * (1.0 / total)
        log_sum = peak * SCALE2 + jnp.log2(total)
        for n in (0, 1):
            os_[yy * 2 + n] = out[:, n * 128 : (n + 1) * 128].astype(BF16)
            ol[yy * 2 + n] = log_sum[:, n * 128 : (n + 1) * 128]

        mine, other = yy * 2 + c, yy * 2 + 1 - c

        @pl.when(k == 0)
        def _():
            pltpu.make_async_copy(os_.at[mine], ro.at[mine], loc.at[1]).start()
            pltpu.make_async_copy(ol.at[mine], rl.at[mine], loc.at[2]).start()

        @pl.when(k > 0)
        def _():
            remote(os_.at[mine], ro.at[p], r1s, r1r, z * NP + mine).start()
            remote(ol.at[mine], rl.at[p], l1s, l1r, z * NP + mine).start()

        remote(os_.at[other], ro.at[p], r1s, r1r, z * NP + other).start()
        remote(ol.at[other], rl.at[p], l1s, l1r, z * NP + other).start()
        return carry

    lax.fori_loop(0, NY, chunk_step, 0)

    wait(sf.at[pl.ds(0, NP - 1)], sfr)
    every_summary = sf[...].reshape(NREQ, HD)
    erow, elane = iota((128, 128), 0), iota((128, 128), 1)
    om_col = jnp.sum(jnp.where(erow == elane, omv, 0), axis=1, keepdims=True)
    tok = iota((1, NREQ), 1)
    tok_slot = ((tok >> 2) & 15) * NP + (tok >> 6)
    tok_super = jnp.sum(jnp.where(om_col == tok_slot, iota((128, NREQ), 0), 0), axis=0, keepdims=True)
    r_head, r_tok = iota((32, NREQ), 0), iota((32, NREQ), 1)
    r_group = (r_head >> 2) & 1
    kept = (r_tok & 3) == r_group
    for j in range(NSEL):
        ids = jnp.where(r_group == 0, siv[0][j], siv[1][j])
        own = jnp.sum(jnp.where(r_tok == me * 4 + (r_head >> 3), ids, 0), axis=1, keepdims=True)
        kept = jnp.logical_and(kept, tok_super != own)
    c_score = dot(qz[z], every_summary, ((1,), (1,))) * SCALE2 + 4.0
    c_score = jnp.where(kept, c_score, NEG)
    c_peak = jnp.max(c_score, axis=1, keepdims=True)
    c_w = jnp.where(kept, jnp.exp2(c_score - c_peak), 0.0)
    c_sum = jnp.sum(c_w, axis=1, keepdims=True)
    c_out = dot(pltpu.roll(c_w, 2, 1).astype(BF16), every_summary)

    wait(os_.at[0], loc.at[1])
    wait(ol.at[0], loc.at[2])
    wait(ro.at[pl.ds(0, NP - 1)], r1r)
    wait(rl.at[pl.ds(0, NP - 1)], l1r)
    l_cols = jnp.transpose(rl[...].reshape(NP, 128), (1, 0))
    peak = jnp.full((1, NREQ), NEG, F32)
    for n in range(NP):
        lse = jnp.where(base == rsel[n : n + 1, :], l_cols[:, n : n + 1], NEG)
        peak = jnp.maximum(peak, jnp.max(lse, axis=0, keepdims=True))
    total = jnp.zeros((1, NREQ), F32)
    merged = jnp.zeros((HD, NREQ), F32)
    for n in range(NP):
        w = jnp.where(base == rsel[n : n + 1, :], jnp.exp2(l_cols[:, n : n + 1] - peak), 0.0)
        total = total + jnp.sum(w, axis=0, keepdims=True)
        merged = merged + dot(ro[n], w.astype(BF16))
    some = total > 0.0
    merged = merged * jnp.where(some, 1.0 / jnp.where(some, total, 1.0), 0.0)
    log_sum = jnp.where(some, peak + jnp.log2(jnp.where(some, total, 1.0)), NEG)
    pzs[...] = jnp.transpose(merged, (1, 0)).astype(BF16).reshape(NZ, 32, HD)
    for n in range(NZ):
        part = log_sum[:, (n // 4) * 128 : (n // 4) * 128 + 128]
        lzs[n] = pltpu.roll(part, 128 - 32 * (n % 4), 1) if n % 4 else part
    keep = [
        pltpu.make_async_copy(pzs.at[z], pz.at[z], loc.at[3]),
        pltpu.make_async_copy(lzs.at[z], lz.at[z], loc.at[4]),
    ]
    for copy in keep:
        copy.start()
    for d in Z_ORDER:
        zz = z_peer(d)
        remote(pzs.at[zz], pz.at[z], r2s, r2r, zz * NP + p).start()
        remote(lzs.at[zz], lz.at[z], l2s, l2r, zz * NP + p).start()
    for copy in keep:
        copy.wait()
    wait(pz.at[pl.ds(0, NZ - 1)], r2r)
    wait(lz.at[pl.ds(0, NZ - 1)], l2r)

    lse = jnp.transpose(lz[...].reshape(NZ, 128), (1, 0))[0:32]
    c_lse = c_peak + jnp.log2(c_sum)
    top = jnp.maximum(jnp.max(lse, axis=1, keepdims=True), c_lse)
    w = jnp.exp2(lse - top)
    c_scale = jnp.exp2(c_peak - top)
    total = jnp.sum(w, axis=1, keepdims=True) + c_scale * c_sum
    result = c_out * c_scale
    for n in range(NZ):
        result = result + pz[n].astype(F32) * w[:, n : n + 1]
    xs[...] = (result / total).astype(BF16).reshape(NX, 8, HD)
    keep = pltpu.make_async_copy(xs.at[rep], o_ref.at[rep], loc.at[5])
    keep.start()
    for d in range(1, NX):
        x = lax.rem(rep + d, NX)
        remote(xs.at[x], o_ref.at[rep], xss, xsr, me, x).start()

    wait(qz.at[pl.ds(0, NZ - 1)], q1s)
    wait(sz.at[pl.ds(0, NZ - 1)], szs)
    wait(qs.at[pl.ds(0, NP - 1)], q2s)
    wait(sf.at[pl.ds(0, NP - 1)], sfs)
    wait(os_.at[pl.ds(0, NP - 1)], r1s)
    wait(ol.at[pl.ds(0, NP - 1)], l1s)
    wait(pzs.at[pl.ds(0, NZ - 1)], r2s)
    wait(lzs.at[pl.ds(0, NZ - 1)], l2s)
    keep.wait()
    wait(xs.at[pl.ds(0, NX - 1)], xss)
    wait(o_ref.at[pl.ds(0, NX - 1)], xsr)


def shards(queries, key_cache, value_cache, summary_keys, summary_values, owner_map, super_ids, fine_ids):
    vmem, dma = pltpu.VMEM, pltpu.SemaphoreType.DMA
    out = pl.pallas_call(
        kernel,
        out_shape=jax.ShapeDtypeStruct((NX, 8, HD), BF16),
        in_specs=[pl.BlockSpec(memory_space=pltpu.HBM)] * 8,
        out_specs=pl.BlockSpec(memory_space=pltpu.VMEM),
        scratch_shapes=[
            vmem((2, HD), BF16),
            vmem((2, HD), BF16),
            vmem((1, 128), I32),
            vmem((2, NSEL, NREQ), I32),
            vmem((2, NFINE, NREQ), I32),
            vmem((SPAN, 2 * HD), BF16),
            vmem((SPAN, 2 * HD), BF16),
            vmem((2 * HD, SPAN), BF16),
            vmem((NZ, 32, HD), BF16),
            vmem((NP, 128, HD), BF16),
            vmem((NP, 128, HD), BF16),
            vmem((NP, NREQ), F32),
            vmem((NY, 32, 256), F32),
            vmem((SPAN, 256), F32),
            vmem((SPAN, 256), BF16),
            vmem((NP, HD, 128), BF16),
            vmem((NP, 1, 128), F32),
            vmem((NP, HD, 128), BF16),
            vmem((NP, 1, 128), F32),
            vmem((NZ, 32, HD), BF16),
            vmem((NZ, 1, 128), F32),
            vmem((NZ, 32, HD), BF16),
            vmem((NZ, 1, 128), F32),
            vmem((NZ, 4, HD), BF16),
            vmem((NZ * 4, HD), F32),
            vmem((NP, NZ * 4, HD), BF16),
            vmem((NX, 8, HD), BF16),
            dma((6,)),
            dma((4,)),
            dma,
            dma,
            dma,
            dma((NY,)),
        ]
        + [dma] * 14
        + [dma((6,))],
        compiler_params=pltpu.CompilerParams(collective_id=0, has_side_effects=True),
    )(
        queries.reshape(32, HD),
        key_cache,
        value_cache,
        summary_keys.reshape(2, HD),
        summary_values.reshape(2, HD),
        owner_map.reshape(1, 128),
        jnp.transpose(super_ids, (1, 2, 0)),
        jnp.transpose(fine_ids, (1, 2, 0)),
    )
    return out.reshape(1, NX * 8, HD)


def solution(mesh):
    in_specs = (
        P("seq", "rep", None),
        P("rep", "seq", None),
        P("rep", "seq", None),
        P("rep", "seq", None),
        P("rep", "seq", None),
        P(),
        P(None, "rep", None),
        P(None, "rep", None),
    )
    return jax.shard_map(
        shards, mesh=mesh, in_specs=in_specs, out_specs=P(("seq", "rep"), None, None), check_vma=False
    )
```

time: 262 us -> 57.1 us (0.22)
  the two profiles are of different devices: /device:TPU:1 before, /device:TPU:2 now
where the time goes in v1:
time: 57.1 us; the launch traced here: 56.9 us
  Pallas kernels  55.6 us (97%)
  local copies, waits for them, and re-layouts  1.3 us (2%)
    pallas_call x1, Pallas kernels, shards(): pl.pallas_call(kernel, out_shape=jax.ShapeDtypeStruct((NX, 8, HD), BF16),...  55.6 us
    unnamed x1, local copies, waits for them, and re-layouts  1.3 us

profile of v1, /device:TPU:2, one launch (start us, length us, event | category | flops | bytes accessed | tf_op | source)
XLA Modules:
  0.0 56.9 jit_solution(12540275628100390328)
XLA Ops:
  0.0 55.6 %shard_map.82 = bf16[4,8,128]{2,1,0:T(8,128)(2,1)} custom-call(bf16[32,128]{1,0:T(8,128)(2,1)} %bitcast.10, bf16[2,2048,128]{2,1,0:T(8,128)(2,1)} %kc_h.1, bf16[2,2048,128]{2,1,0:T(8,128)(2,1)} %vc_h.1, bf16[2,128]{1,0:T(2,128)(2,1)} %bitcast.11, bf16[2,128]{1,0:T(2,128)(2,1)} %bitcast.12, s32[1,128]{1,0:T(1,128)} %bitcast.13, s32[2,4,512]{2,1,0:T(4,128)} %bitcast.9, ...), custom_call_target="tpu_custom_call" | custom-call | tf_op jit(solution)/shard_map/pallas_call | solution.py:318
  55.6 1.3 %copy.10 = bf16[1,32,128]{2,1,0:T(8,128)(2,1)} copy(bf16[1,32,128]{2,1,0:T(8,128)(2,1)} %bitcast.8) | data formatting | bytes 16384

commit v2 on v1

--- a/solution.py
+++ b/solution.py
@@ -16,6 +16,7 @@
 NEG = -1e30
 SCALE2 = HD**-0.5 / math.log(2.0)
 Z_ORDER = (8, 7, 9, 6, 10, 5, 11, 4, 12, 3, 13, 2, 14, 1, 15)
+PLANE = ((2, 0), (2, 1), (1, 0), (1, 1), (3, 0), (3, 1), (0, 1), (0, 0))
 
 
 def iota(shape, dim):
@@ -42,7 +43,7 @@
 
 def kernel(
     q_h, kc_h, vc_h, sk_h, sv_h, om_h, si_h, fi_h, o_ref,
-    sk, sv, om, si, fi, kcat, vcat, v_t, qz, qs, rq, rsel, meta, s_s, p_s,
+    sk, sv, om, si, fi, kcat, vcat, v_t, qz, qs, rq, rsel, meta, flag, pick, w_s, s_s, p_s,
     os_, ol, ro, rl, pzs, lzs, pz, lz, sz, szf, sf, xs,
     load_sem, kv_sem, q1s, q1r, q2s, q2r, r1s, r1r, l1s, l1r, r2s, r2r, l2s, l2r, szs, szr, sfs, sfr, xss, xsr, loc,
 ):
@@ -56,7 +57,7 @@
     def plane_peer(dy, dc):
         return lax.rem(y + dy, NY) * 2 + lax.rem(c + dc, 2)
 
-    plane = [(dy, dc) for dy in (2, 1, 3, 0) for dc in (0, 1) if dy or dc]
+    plane = PLANE[:-1]
 
     barrier = pltpu.get_barrier_semaphore()
     for d in Z_ORDER:
@@ -94,8 +95,6 @@
 
     for d in Z_ORDER:
         remote(qz.at[z], qz.at[z], q1s, q1r, z_peer(d) * NP + p).start()
-    for d in Z_ORDER:
-        remote(sz.at[z], sz.at[z], szs, szr, z_peer(d) * NP + p).start()
 
     omv = om[...]
     siv = [[si[g, j : j + 1, :] for j in range(NSEL)] for g in (0, 1)]
@@ -147,36 +146,43 @@
             at = jnp.where(((col >> 2) & 1) == slot, sender, -1)
             acc = acc + dot(stacked[slot], jnp.where((row >> 2) == at, 1.0, 0.0).astype(BF16))
         meta[chunk] = acc
-
-    srow, slane = iota((128, NREQ), 0), iota((128, NREQ), 1)
+        flag[chunk] = jnp.transpose(acc[16:24], (1, 0))
+
+    brow, blane = iota((32, 128), 0), iota((32, 128), 1)
     base = jnp.where(
-        jnp.logical_and((srow >> 3) == (slane >> 5), (srow & 3) == (slane & 3)), ((srow >> 2) & 1) + 1, -1
+        jnp.logical_and((brow >> 3) == (blane >> 5), (brow & 3) == (blane & 3)), ((brow >> 2) & 1) + 1, -1
     ).astype(F32)
-
-    wait(qz.at[pl.ds(0, NZ - 1)], q1r)
-    every = qz[...].reshape(NREQ, HD)
-    for dy, dc in [(0, 0)] + plane:
-        peer = plane_peer(dy, dc)
-        choose = jnp.where(base == rsel[pl.ds(peer, 1), :], 1.0, 0.0).astype(BF16)
-        qs[peer] = dot(choose, every).astype(BF16)
-        if dy or dc:
-            remote(qs.at[peer], rq.at[p], q2s, q2r.at[dy], z * NP + peer).start()
-        else:
-            pltpu.make_async_copy(qs.at[peer], rq.at[peer], loc.at[0]).start()
-
-    wait(sz.at[pl.ds(0, NZ - 1)], szr)
-    for n in range(NZ):
-        szf[n * 4 : n * 4 + 4, :] = sz[n].astype(F32)
-    sf[p] = szf[...].astype(BF16)
-    for dy, dc in plane:
-        remote(sf.at[p], sf.at[p], sfs, sfr, z * NP + plane_peer(dy, dc)).start()
-
+    pick[...] = jnp.zeros_like(pick)
+    w_s[...] = jnp.zeros_like(w_s)
+    for n, (dy, dc) in enumerate(PLANE):
+        code = rsel[pl.ds(plane_peer(dy, dc), 1), :]
+        for b in range(4):
+            same = base == code[:, b * 128 : (b + 1) * 128]
+            pick[n * 128 + b * 32 : n * 128 + (b + 1) * 32, b * 128 : (b + 1) * 128] = jnp.where(
+                same, 1.0, 0.0
+            ).astype(BF16)
     for copy in kv_loads:
         copy.wait()
     v_t[...] = jnp.transpose(vcat[...], (1, 0))
+
+    wait(qz.at[pl.ds(0, NZ - 1)], q1r)
+    every = qz[...].reshape(NREQ, HD)
+    for half in (0, 1):
+        rows = dot(pick[half * 512 : (half + 1) * 512, :], every).astype(BF16)
+        qs[half * 4 : half * 4 + 4] = rows.reshape(4, 128, HD)
+        for n in range(half * 4, half * 4 + 4):
+            dy, dc = PLANE[n]
+            if dy or dc:
+                remote(qs.at[n], rq.at[p], q2s, q2r.at[dy], z * NP + plane_peer(dy, dc)).start()
+            else:
+                pltpu.make_async_copy(qs.at[n], rq.at[p], loc.at[0]).start()
+    for d in Z_ORDER:
+        remote(sz.at[z], sz.at[z], szs, szr, z_peer(d) * NP + p).start()
     wait(qs.at[0], loc.at[0])
 
-    def chunk_step(k, carry):
+    def chunk_step(turn, carry):
+        k = jnp.where(turn == 2, 3, jnp.where(turn == 3, 2, turn))
+
         @pl.when(k == 0)
         def _():
             wait(rq.at[0], q2r.at[0])
@@ -187,7 +193,7 @@
 
         yy = lax.rem(y + NY - k, NY)
         m_all = meta[yy]
-        flags = jnp.transpose(m_all[16:24], (1, 0)).astype(BF16)
+        flags = flag[yy].astype(BF16)
         rows = rq[pl.ds(yy * 2, 2)].reshape(256, HD)
         split = jnp.concatenate([rows * flags[:, 0:1], rows * flags[:, 1:2]], axis=1)
         s_s[...] = dot(kcat[...], split, ((1,), (1,)))
@@ -225,6 +231,57 @@
         return carry
 
     lax.fori_loop(0, NY, chunk_step, 0)
+
+    wait(sz.at[pl.ds(0, NZ - 1)], szr)
+    for n in range(NZ):
+        szf[n * 4 : n * 4 + 4, :] = sz[n].astype(F32)
+    sf[p] = szf[...].astype(BF16)
+    for dy, dc in plane:
+        remote(sf.at[p], sf.at[p], sfs, sfr, z * NP + plane_peer(dy, dc)).start()
+
+    wait(os_.at[0], loc.at[1])
+    wait(ol.at[0], loc.at[2])
+    wait(ro.at[pl.ds(0, NP - 1)], r1r)
+    wait(rl.at[pl.ds(0, NP - 1)], l1r)
+    l_cols = jnp.transpose(rl[...].reshape(NP, 128), (1, 0))
+    same = [[base == rsel[n : n + 1, b * 128 : (b + 1) * 128] for b in range(4)] for n in range(NP)]
+    peaks, totals = [], []
+    for b in range(4):
+        peak = jnp.full((32, 128), NEG, F32)
+        for n in range(NP):
+            peak = jnp.maximum(peak, jnp.where(same[n][b], l_cols[b * 32 : (b + 1) * 32, n : n + 1], NEG))
+        peak = jnp.max(peak, axis=0, keepdims=True)
+        total = jnp.zeros((32, 128), F32)
+        for n in range(NP):
+            w = jnp.where(same[n][b], jnp.exp2(l_cols[b * 32 : (b + 1) * 32, n : n + 1] - peak), 0.0)
+            total = total + w
+            w_s[n * 128 + b * 32 : n * 128 + (b + 1) * 32, b * 128 : (b + 1) * 128] = w.astype(BF16)
+        peaks.append(peak)
+        totals.append(jnp.sum(total, axis=0, keepdims=True))
+    peak, total = jnp.concatenate(peaks, axis=1), jnp.concatenate(totals, axis=1)
+    merged = jnp.zeros((HD, NREQ), F32)
+    for n in range(0, NP, 2):
+        pair = jnp.concatenate([ro[n], ro[n + 1]], axis=1)
+        merged = merged + dot(pair, w_s[n * 128 : (n + 2) * 128, :])
+    some = total > 0.0
+    merged = merged * jnp.where(some, 1.0 / jnp.where(some, total, 1.0), 0.0)
+    log_sum = jnp.where(some, peak + jnp.log2(jnp.where(some, total, 1.0)), NEG)
+    pzs[...] = jnp.transpose(merged, (1, 0)).astype(BF16).reshape(NZ, 32, HD)
+    for n in range(NZ):
+        part = log_sum[:, (n // 4) * 128 : (n // 4) * 128 + 128]
+        lzs[n] = pltpu.roll(part, 128 - 32 * (n % 4), 1) if n % 4 else part
+    keep = [
+        pltpu.make_async_copy(pzs.at[z], pz.at[z], loc.at[3]),
+        pltpu.make_async_copy(lzs.at[z], lz.at[z], loc.at[4]),
+    ]
+    for copy in keep:
+        copy.start()
+    for d in Z_ORDER:
+        zz = z_peer(d)
+        remote(pzs.at[zz], pz.at[z], r2s, r2r, zz * NP + p).start()
+        remote(lzs.at[zz], lz.at[z], l2s, l2r, zz * NP + p).start()
+    for copy in keep:
+        copy.wait()
 
     wait(sf.at[pl.ds(0, NP - 1)], sfr)
     every_summary = sf[...].reshape(NREQ, HD)
@@ -247,40 +304,6 @@
     c_sum = jnp.sum(c_w, axis=1, keepdims=True)
     c_out = dot(pltpu.roll(c_w, 2, 1).astype(BF16), every_summary)
 
-    wait(os_.at[0], loc.at[1])
-    wait(ol.at[0], loc.at[2])
-    wait(ro.at[pl.ds(0, NP - 1)], r1r)
-    wait(rl.at[pl.ds(0, NP - 1)], l1r)
-    l_cols = jnp.transpose(rl[...].reshape(NP, 128), (1, 0))
-    peak = jnp.full((1, NREQ), NEG, F32)
-    for n in range(NP):
-        lse = jnp.where(base == rsel[n : n + 1, :], l_cols[:, n : n + 1], NEG)
-        peak = jnp.maximum(peak, jnp.max(lse, axis=0, keepdims=True))
-    total = jnp.zeros((1, NREQ), F32)
-    merged = jnp.zeros((HD, NREQ), F32)
-    for n in range(NP):
-        w = jnp.where(base == rsel[n : n + 1, :], jnp.exp2(l_cols[:, n : n + 1] - peak), 0.0)
-        total = total + jnp.sum(w, axis=0, keepdims=True)
-        merged = merged + dot(ro[n], w.astype(BF16))
-    some = total > 0.0
-    merged = merged * jnp.where(some, 1.0 / jnp.where(some, total, 1.0), 0.0)
-    log_sum = jnp.where(some, peak + jnp.log2(jnp.where(some, total, 1.0)), NEG)
-    pzs[...] = jnp.transpose(merged, (1, 0)).astype(BF16).reshape(NZ, 32, HD)
-    for n in range(NZ):
-        part = log_sum[:, (n // 4) * 128 : (n // 4) * 128 + 128]
-        lzs[n] = pltpu.roll(part, 128 - 32 * (n % 4), 1) if n % 4 else part
-    keep = [
-        pltpu.make_async_copy(pzs.at[z], pz.at[z], loc.at[3]),
-        pltpu.make_async_copy(lzs.at[z], lz.at[z], loc.at[4]),
-    ]
-    for copy in keep:
-        copy.start()
-    for d in Z_ORDER:
-        zz = z_peer(d)
-        remote(pzs.at[zz], pz.at[z], r2s, r2r, zz * NP + p).start()
-        remote(lzs.at[zz], lz.at[z], l2s, l2r, zz * NP + p).start()
-    for copy in keep:
-        copy.wait()
     wait(pz.at[pl.ds(0, NZ - 1)], r2r)
     wait(lz.at[pl.ds(0, NZ - 1)], l2r)
 
@@ -334,6 +357,9 @@
             vmem((NP, 128, HD), BF16),
             vmem((NP, NREQ), F32),
             vmem((NY, 32, 256), F32),
+            vmem((NY, 256, 8), F32),
+            vmem((NP * 128, NREQ), BF16),
+            vmem((NP * 128, NREQ), BF16),
             vmem((SPAN, 256), F32),
             vmem((SPAN, 256), BF16),
             vmem((NP, HD, 128), BF16),

time: 57.1 us -> 55.4 us (0.970)
  the two profiles are of different devices: /device:TPU:2 before, /device:TPU:16 now
where the time goes in v2:
time: 55.4 us; the launch traced here: 55.2 us
  Pallas kernels  53.9 us (97%)
  local copies, waits for them, and re-layouts  1.3 us (2%)
    pallas_call x1, Pallas kernels, shards(): pl.pallas_call(kernel, out_shape=jax.ShapeDtypeStruct((NX, 8, HD), BF16),...  53.9 us
    unnamed x1, local copies, waits for them, and re-layouts  1.3 us

profile of v2, /device:TPU:16, one launch (start us, length us, event | category | flops | bytes accessed | tf_op | source)
XLA Modules:
  0.0 55.2 jit_solution(17961670529008670779)
XLA Ops:
  0.0 53.9 %shard_map.82 = bf16[4,8,128]{2,1,0:T(8,128)(2,1)} custom-call(bf16[32,128]{1,0:T(8,128)(2,1)} %bitcast.10, bf16[2,2048,128]{2,1,0:T(8,128)(2,1)} %kc_h.1, bf16[2,2048,128]{2,1,0:T(8,128)(2,1)} %vc_h.1, bf16[2,128]{1,0:T(2,128)(2,1)} %bitcast.11, bf16[2,128]{1,0:T(2,128)(2,1)} %bitcast.12, s32[1,128]{1,0:T(1,128)} %bitcast.13, s32[2,4,512]{2,1,0:T(4,128)} %bitcast.9, ...), custom_call_target="tpu_custom_call" | custom-call | tf_op jit(solution)/shard_map/pallas_call | solution.py:341
  53.9 1.3 %copy.10 = bf16[1,32,128]{2,1,0:T(8,128)(2,1)} copy(bf16[1,32,128]{2,1,0:T(8,128)(2,1)} %bitcast.8) | data formatting | bytes 16384

commit v3 on v2

--- a/solution.py
+++ b/solution.py
@@ -16,6 +16,7 @@
 NEG = -1e30
 SCALE2 = HD**-0.5 / math.log(2.0)
 Z_ORDER = (8, 7, 9, 6, 10, 5, 11, 4, 12, 3, 13, 2, 14, 1, 15)
+PARTS = 4
 PLANE = ((2, 0), (2, 1), (1, 0), (1, 1), (3, 0), (3, 1), (0, 1), (0, 0))
 
 
@@ -43,7 +44,7 @@
 
 def kernel(
     q_h, kc_h, vc_h, sk_h, sv_h, om_h, si_h, fi_h, o_ref,
-    sk, sv, om, si, fi, kcat, vcat, v_t, qz, qs, rq, rsel, meta, flag, pick, w_s, s_s, p_s,
+    sk, sv, om, si, fi, kcat, vcat, v_t, qz, qs, rq, rsel, meta, flag, pick, w_s,
     os_, ol, ro, rl, pzs, lzs, pz, lz, sz, szf, sf, xs,
     load_sem, kv_sem, q1s, q1r, q2s, q2r, r1s, r1r, l1s, l1r, r2s, r2r, l2s, l2r, szs, szr, sfs, sfr, xss, xsr, loc,
 ):
@@ -196,18 +197,27 @@
         flags = flag[yy].astype(BF16)
         rows = rq[pl.ds(yy * 2, 2)].reshape(256, HD)
         split = jnp.concatenate([rows * flags[:, 0:1], rows * flags[:, 1:2]], axis=1)
-        s_s[...] = dot(kcat[...], split, ((1,), (1,)))
         bias = jnp.where(m_all[0:16] > 0.5, 0.0, NEG)
-        peak = jnp.full((1, 256), -3e38, F32)
-        for b in range(SUPER):
-            top = jnp.max(s_s[b * BLK : (b + 1) * BLK, :], axis=0, keepdims=True)
-            peak = jnp.maximum(peak, top + bias[b : b + 1])
-        total = jnp.zeros((1, 256), F32)
-        for b in range(SUPER):
-            w = jnp.exp2((s_s[b * BLK : (b + 1) * BLK, :] + (bias[b : b + 1] - peak)) * SCALE2)
-            total = total + jnp.sum(w, axis=0, keepdims=True)
-            p_s[b * BLK : (b + 1) * BLK, :] = w.astype(BF16)
-        out = dot(v_t[...], p_s[...])
+        span, per = SPAN // PARTS, SUPER // PARTS
+        outs, peaks, totals = [], [], []
+        for t in range(PARTS):
+            s = dot(kcat[t * span : (t + 1) * span, :], split, ((1,), (1,)))
+            top = jnp.full((1, 256), -3e38, F32)
+            for b in range(per):
+                one = jnp.max(s[b * BLK : (b + 1) * BLK], axis=0, keepdims=True)
+                top = jnp.maximum(top, one + bias[t * per + b : t * per + b + 1])
+            part, ws = jnp.zeros((1, 256), F32), []
+            for b in range(per):
+                w = jnp.exp2((s[b * BLK : (b + 1) * BLK] + (bias[t * per + b : t * per + b + 1] - top)) * SCALE2)
+                part = part + jnp.sum(w, axis=0, keepdims=True)
+                ws.append(w.astype(BF16))
+            outs.append(dot(v_t[:, t * span : (t + 1) * span], jnp.concatenate(ws, axis=0)))
+            peaks.append(top)
+            totals.append(part)
+        peak = functools.reduce(jnp.maximum, peaks)
+        factors = [jnp.exp2((top - peak) * SCALE2) for top in peaks]
+        total = sum(f * part for f, part in zip(factors, totals))
+        out = sum(f * o for f, o in zip(factors, outs))
         out = jnp.where(m_all[17:18] > 0.5, out[HD : 2 * HD], out[0:HD]) * (1.0 / total)
         log_sum = peak * SCALE2 + jnp.log2(total)
         for n in (0, 1):
@@ -342,7 +352,7 @@
         kernel,
         out_shape=jax.ShapeDtypeStruct((NX, 8, HD), BF16),
         in_specs=[pl.BlockSpec(memory_space=pltpu.HBM)] * 8,
-        out_specs=pl.BlockSpec(memory_space=pltpu.VMEM),
+        out_specs=pl.BlockSpec(memory_space=pltpu.HBM),
         scratch_shapes=[
             vmem((2, HD), BF16),
             vmem((2, HD), BF16),
@@ -360,8 +370,6 @@
             vmem((NY, 256, 8), F32),
             vmem((NP * 128, NREQ), BF16),
             vmem((NP * 128, NREQ), BF16),
-            vmem((SPAN, 256), F32),
-            vmem((SPAN, 256), BF16),
             vmem((NP, HD, 128), BF16),
             vmem((NP, 1, 128), F32),
             vmem((NP, HD, 128), BF16),

time: 55.4 us -> 54.2 us (0.978)
  the two profiles are of different devices: /device:TPU:16 before, /device:TPU:1 now
where the time goes in v3:
time: 54.2 us; the launch traced here: 54 us
  Pallas kernels  52.7 us (97%)
  local copies, waits for them, and re-layouts  1.3 us (2%)
    pallas_call x1, Pallas kernels, shards(): pl.pallas_call(kernel, out_shape=jax.ShapeDtypeStruct((NX, 8, HD), BF16),...  52.7 us
    unnamed x1, local copies, waits for them, and re-layouts  1.3 us

profile of v3, /device:TPU:1, one launch (start us, length us, event | category | flops | bytes accessed | tf_op | source)
XLA Modules:
  0.0 54.0 jit_solution(8840907199514727513)
XLA Ops:
  0.0 52.7 %shard_map.82 = bf16[4,8,128]{2,1,0:T(8,128)(2,1)} custom-call(bf16[32,128]{1,0:T(8,128)(2,1)} %bitcast.10, bf16[2,2048,128]{2,1,0:T(8,128)(2,1)} %kc_h.1, bf16[2,2048,128]{2,1,0:T(8,128)(2,1)} %vc_h.1, bf16[2,128]{1,0:T(2,128)(2,1)} %bitcast.11, bf16[2,128]{1,0:T(2,128)(2,1)} %bitcast.12, s32[1,128]{1,0:T(1,128)} %bitcast.13, s32[2,4,512]{2,1,0:T(4,128)} %bitcast.9, ...), custom_call_target="tpu_custom_call" | custom-call | tf_op jit(solution)/shard_map/pallas_call | solution.py:351
  52.7 1.3 %copy.10 = bf16[1,32,128]{2,1,0:T(8,128)(2,1)} copy(bf16[1,32,128]{2,1,0:T(8,128)(2,1)} %bitcast.8) | data formatting | bytes 16384

commit v4 on v3

--- a/solution.py
+++ b/solution.py
@@ -16,7 +16,8 @@
 NEG = -1e30
 SCALE2 = HD**-0.5 / math.log(2.0)
 Z_ORDER = (8, 7, 9, 6, 10, 5, 11, 4, 12, 3, 13, 2, 14, 1, 15)
-PARTS = 4
+PARTS = 1
+NEAR = 4
 PLANE = ((2, 0), (2, 1), (1, 0), (1, 1), (3, 0), (3, 1), (0, 1), (0, 0))
 
 
@@ -79,7 +80,7 @@
 
     loads = [
         pltpu.make_async_copy(a, b, load_sem.at[n])
-        for n, (a, b) in enumerate([(q_h, qz.at[z]), (sk_h, sk), (sv_h, sv), (om_h, om), (si_h, si), (fi_h, fi)])
+        for n, (a, b) in enumerate([(q_h, qz.at[NEAR]), (sk_h, sk), (sv_h, sv), (om_h, om), (si_h, si), (fi_h, fi)])
     ]
     kv_loads = [
         pltpu.make_async_copy(a.at[g], b.at[:, pl.ds(g * HD, HD)], kv_sem.at[2 * n + g])
@@ -95,7 +96,8 @@
     pl.semaphore_wait(barrier, len(Z_ORDER) + len(plane) + NX - 1)
 
     for d in Z_ORDER:
-        remote(qz.at[z], qz.at[z], q1s, q1r, z_peer(d) * NP + p).start()
+        e = (NEAR - d) % NZ
+        remote(qz.at[NEAR], qz.at[e], q1s, q1r.at[e // 8], z_peer(d) * NP + p).start()
 
     omv = om[...]
     siv = [[si[g, j : j + 1, :] for j in range(NSEL)] for g in (0, 1)]
@@ -109,7 +111,7 @@
         hits.append(jnp.where(h, 1, 0))
     ranks = group_rank(hits)
     row, lane = iota((NREQ, NREQ), 0), iota((NREQ, NREQ), 1)
-    source = (lane >> 5) * 32 + p * 4 + ((lane >> 3) & 3)
+    source = (((lane >> 5) + z + NZ - NEAR) & 15) * 32 + p * 4 + ((lane >> 3) & 3)
     picked = jnp.zeros((NP, NREQ), F32)
     for g in (0, 1):
         spread = jnp.where(row == jnp.where(((lane >> 2) & 1) == g, source, -1), 1.0, 0.0).astype(BF16)
@@ -139,9 +141,11 @@
         wanted = own_bits[0] * use[0][0:1] + own_bits[1] * use[1][0:1]
         flags = jnp.where(sub8 == 0, use[0], jnp.where(sub8 == 1, use[1], 0.0))
         stacked.append(jnp.concatenate([wanted, flags, jnp.zeros((8, NREQ), F32)], axis=0).astype(BF16))
-    for chunk in range(NY):
+    for chunk in range(4):
         row, col = iota((NREQ, 256), 0), iota((NREQ, 256), 1)
-        sender = ((col >> 3) & 15) * NP + chunk * 2 + (col >> 7)
+        place = (chunk // 2) * 8 + ((col >> 3) & 7)
+        chip = (y + NY - (chunk % 2) * 2 - (col >> 7)) & 3
+        sender = ((place + z + NZ - NEAR) & 15) * NP + chip * 2 + ((col >> 6) & 1)
         acc = jnp.zeros((32, 256), F32)
         for slot in (0, 1):
             at = jnp.where(((col >> 2) & 1) == slot, sender, -1)
@@ -159,59 +163,50 @@
         code = rsel[pl.ds(plane_peer(dy, dc), 1), :]
         for b in range(4):
             same = base == code[:, b * 128 : (b + 1) * 128]
-            pick[n * 128 + b * 32 : n * 128 + (b + 1) * 32, b * 128 : (b + 1) * 128] = jnp.where(
-                same, 1.0, 0.0
-            ).astype(BF16)
+            at = (b // 2) * 512 + n * 64 + (b % 2) * 32
+            pick[at : at + 32, (b % 2) * 128 : (b % 2) * 128 + 128] = jnp.where(same, 1.0, 0.0).astype(BF16)
     for copy in kv_loads:
         copy.wait()
     v_t[...] = jnp.transpose(vcat[...], (1, 0))
 
-    wait(qz.at[pl.ds(0, NZ - 1)], q1r)
-    every = qz[...].reshape(NREQ, HD)
-    for half in (0, 1):
-        rows = dot(pick[half * 512 : (half + 1) * 512, :], every).astype(BF16)
-        qs[half * 4 : half * 4 + 4] = rows.reshape(4, 128, HD)
-        for n in range(half * 4, half * 4 + 4):
-            dy, dc = PLANE[n]
+    for t in (0, 1):
+        wait(qz.at[pl.ds(0, 7 + t)], q1r.at[t])
+        every = qz[t * 8 : (t + 1) * 8].reshape(256, HD)
+        rows = dot(pick[t * 512 : (t + 1) * 512, :], every).astype(BF16)
+        qs[t] = rows.reshape(NP, 64, HD)
+        for n, (dy, dc) in enumerate(PLANE):
             if dy or dc:
-                remote(qs.at[n], rq.at[p], q2s, q2r.at[dy], z * NP + plane_peer(dy, dc)).start()
+                remote(
+                    qs.at[t, n], rq.at[t, dy * 2 + c], q2s, q2r.at[t, dy // 2], z * NP + plane_peer(dy, dc)
+                ).start()
             else:
-                pltpu.make_async_copy(qs.at[n], rq.at[p], loc.at[0]).start()
+                pltpu.make_async_copy(qs.at[t, n], rq.at[t, c], loc.at[t]).start()
     for d in Z_ORDER:
         remote(sz.at[z], sz.at[z], szs, szr, z_peer(d) * NP + p).start()
-    wait(qs.at[0], loc.at[0])
-
-    def chunk_step(turn, carry):
-        k = jnp.where(turn == 2, 3, jnp.where(turn == 3, 2, turn))
-
-        @pl.when(k == 0)
-        def _():
-            wait(rq.at[0], q2r.at[0])
-
-        @pl.when(k > 0)
-        def _():
-            wait(rq.at[pl.ds(0, 2)], q2r.at[k])
-
-        yy = lax.rem(y + NY - k, NY)
-        m_all = meta[yy]
-        flags = flag[yy].astype(BF16)
-        rows = rq[pl.ds(yy * 2, 2)].reshape(256, HD)
+
+    def batch_step(t, carry):
+        wait(rq.at[0, 0], loc.at[t])
+        wait(rq.at[0, pl.ds(0, 3)], q2r.at[t, 0])
+        wait(rq.at[0, pl.ds(0, 4)], q2r.at[t, 1])
+        m_all = jnp.concatenate([meta[t * 2], meta[t * 2 + 1]], axis=1)
+        flags = jnp.concatenate([flag[t * 2], flag[t * 2 + 1]], axis=0).astype(BF16)
+        rows = rq[t].reshape(NREQ, HD)
         split = jnp.concatenate([rows * flags[:, 0:1], rows * flags[:, 1:2]], axis=1)
         bias = jnp.where(m_all[0:16] > 0.5, 0.0, NEG)
         span, per = SPAN // PARTS, SUPER // PARTS
         outs, peaks, totals = [], [], []
-        for t in range(PARTS):
-            s = dot(kcat[t * span : (t + 1) * span, :], split, ((1,), (1,)))
-            top = jnp.full((1, 256), -3e38, F32)
+        for g in range(PARTS):
+            s = dot(kcat[g * span : (g + 1) * span, :], split, ((1,), (1,)))
+            top = jnp.full((1, NREQ), -3e38, F32)
             for b in range(per):
                 one = jnp.max(s[b * BLK : (b + 1) * BLK], axis=0, keepdims=True)
-                top = jnp.maximum(top, one + bias[t * per + b : t * per + b + 1])
-            part, ws = jnp.zeros((1, 256), F32), []
+                top = jnp.maximum(top, one + bias[g * per + b : g * per + b + 1])
+            part, ws = jnp.zeros((1, NREQ), F32), []
             for b in range(per):
-                w = jnp.exp2((s[b * BLK : (b + 1) * BLK] + (bias[t * per + b : t * per + b + 1] - top)) * SCALE2)
+                w = jnp.exp2((s[b * BLK : (b + 1) * BLK] + (bias[g * per + b : g * per + b + 1] - top)) * SCALE2)
                 part = part + jnp.sum(w, axis=0, keepdims=True)
                 ws.append(w.astype(BF16))
-            outs.append(dot(v_t[:, t * span : (t + 1) * span], jnp.concatenate(ws, axis=0)))
+            outs.append(dot(v_t[:, g * span : (g + 1) * span], jnp.concatenate(ws, axis=0)))
             peaks.append(top)
             totals.append(part)
         peak = functools.reduce(jnp.maximum, peaks)
@@ -219,28 +214,24 @@
         total = sum(f * part for f, part in zip(factors, totals))
         out = sum(f * o for f, o in zip(factors, outs))
         out = jnp.where(m_all[17:18] > 0.5, out[HD : 2 * HD], out[0:HD]) * (1.0 / total)
+        out = jnp.transpose(out, (1, 0)).astype(BF16)
+        os_[t] = out.reshape(NP, 64, HD)
         log_sum = peak * SCALE2 + jnp.log2(total)
-        for n in (0, 1):
-            os_[yy * 2 + n] = out[:, n * 128 : (n + 1) * 128].astype(BF16)
-            ol[yy * 2 + n] = log_sum[:, n * 128 : (n + 1) * 128]
-
-        mine, other = yy * 2 + c, yy * 2 + 1 - c
-
-        @pl.when(k == 0)
-        def _():
-            pltpu.make_async_copy(os_.at[mine], ro.at[mine], loc.at[1]).start()
-            pltpu.make_async_copy(ol.at[mine], rl.at[mine], loc.at[2]).start()
-
-        @pl.when(k > 0)
-        def _():
-            remote(os_.at[mine], ro.at[p], r1s, r1r, z * NP + mine).start()
-            remote(ol.at[mine], rl.at[p], l1s, l1r, z * NP + mine).start()
-
-        remote(os_.at[other], ro.at[p], r1s, r1r, z * NP + other).start()
-        remote(ol.at[other], rl.at[p], l1s, l1r, z * NP + other).start()
+        for a in range(NP):
+            part = log_sum[:, (a // 2) * 128 : (a // 2) * 128 + 128]
+            ol[t, a] = pltpu.roll(part, 64, 1) if a % 2 else part
+        for k in (2, 1, 3):
+            for core in (0, 1):
+                peer = z * NP + lax.rem(y + NY - k, NY) * 2 + core
+                remote(ol.at[t, k * 2 + core], rl.at[t, p], l1s, l1r.at[t], peer).start()
+                remote(os_.at[t, k * 2 + core], ro.at[t, p], r1s, r1r.at[t], peer).start()
+        remote(os_.at[t, 1 - c], ro.at[t, p], r1s, r1r.at[t], z * NP + y * 2 + 1 - c).start()
+        remote(ol.at[t, 1 - c], rl.at[t, p], l1s, l1r.at[t], z * NP + y * 2 + 1 - c).start()
+        pltpu.make_async_copy(os_.at[t, c], ro.at[t, p], loc.at[2 + t]).start()
+        pltpu.make_async_copy(ol.at[t, c], rl.at[t, p], loc.at[4 + t]).start()
         return carry
 
-    lax.fori_loop(0, NY, chunk_step, 0)
+    lax.fori_loop(0, 2, batch_step, 0)
 
     wait(sz.at[pl.ds(0, NZ - 1)], szr)
     for n in range(NZ):
@@ -249,47 +240,47 @@
     for dy, dc in plane:
         remote(sf.at[p], sf.at[p], sfs, sfr, z * NP + plane_peer(dy, dc)).start()
 
-    wait(os_.at[0], loc.at[1])
-    wait(ol.at[0], loc.at[2])
-    wait(ro.at[pl.ds(0, NP - 1)], r1r)
-    wait(rl.at[pl.ds(0, NP - 1)], l1r)
-    l_cols = jnp.transpose(rl[...].reshape(NP, 128), (1, 0))
-    same = [[base == rsel[n : n + 1, b * 128 : (b + 1) * 128] for b in range(4)] for n in range(NP)]
-    peaks, totals = [], []
-    for b in range(4):
-        peak = jnp.full((32, 128), NEG, F32)
-        for n in range(NP):
-            peak = jnp.maximum(peak, jnp.where(same[n][b], l_cols[b * 32 : (b + 1) * 32, n : n + 1], NEG))
-        peak = jnp.max(peak, axis=0, keepdims=True)
-        total = jnp.zeros((32, 128), F32)
-        for n in range(NP):
-            w = jnp.where(same[n][b], jnp.exp2(l_cols[b * 32 : (b + 1) * 32, n : n + 1] - peak), 0.0)
-            total = total + w
-            w_s[n * 128 + b * 32 : n * 128 + (b + 1) * 32, b * 128 : (b + 1) * 128] = w.astype(BF16)
-        peaks.append(peak)
-        totals.append(jnp.sum(total, axis=0, keepdims=True))
-    peak, total = jnp.concatenate(peaks, axis=1), jnp.concatenate(totals, axis=1)
-    merged = jnp.zeros((HD, NREQ), F32)
-    for n in range(0, NP, 2):
-        pair = jnp.concatenate([ro[n], ro[n + 1]], axis=1)
-        merged = merged + dot(pair, w_s[n * 128 : (n + 2) * 128, :])
-    some = total > 0.0
-    merged = merged * jnp.where(some, 1.0 / jnp.where(some, total, 1.0), 0.0)
-    log_sum = jnp.where(some, peak + jnp.log2(jnp.where(some, total, 1.0)), NEG)
-    pzs[...] = jnp.transpose(merged, (1, 0)).astype(BF16).reshape(NZ, 32, HD)
-    for n in range(NZ):
-        part = log_sum[:, (n // 4) * 128 : (n // 4) * 128 + 128]
-        lzs[n] = pltpu.roll(part, 128 - 32 * (n % 4), 1) if n % 4 else part
     keep = [
-        pltpu.make_async_copy(pzs.at[z], pz.at[z], loc.at[3]),
-        pltpu.make_async_copy(lzs.at[z], lz.at[z], loc.at[4]),
+        pltpu.make_async_copy(pzs.at[NEAR], pz.at[z], loc.at[6]),
+        pltpu.make_async_copy(lzs.at[NEAR], lz.at[z], loc.at[7]),
     ]
-    for copy in keep:
-        copy.start()
-    for d in Z_ORDER:
-        zz = z_peer(d)
-        remote(pzs.at[zz], pz.at[z], r2s, r2r, zz * NP + p).start()
-        remote(lzs.at[zz], lz.at[z], l2s, l2r, zz * NP + p).start()
+    for t in (0, 1):
+        wait(os_.at[0, 0], loc.at[2 + t])
+        wait(ol.at[0, 0], loc.at[4 + t])
+        wait(rl.at[0, pl.ds(0, NP - 1)], l1r.at[t])
+        l_cols = jnp.transpose(rl[t].reshape(NP, 128), (1, 0))
+        for b in (0, 1):
+            at = (t * 2 + b) * 128
+            same = [base == rsel[n : n + 1, at : at + 128] for n in range(NP)]
+            cols = l_cols[b * 32 : (b + 1) * 32]
+            peak = jnp.full((32, 128), NEG, F32)
+            for n in range(NP):
+                peak = jnp.maximum(peak, jnp.where(same[n], cols[:, n : n + 1], NEG))
+            peak = jnp.max(peak, axis=0, keepdims=True)
+            ws = [jnp.where(same[n], jnp.exp2(cols[:, n : n + 1] - peak), 0.0) for n in range(NP)]
+            total = jnp.sum(sum(ws), axis=0, keepdims=True)
+            some = total > 0.0
+            filled = jnp.where(some, total, 1.0)
+            inverse = jnp.where(some, 1.0 / filled, 0.0)
+            for n in range(NP):
+                w_s[t, n * 64 + b * 32 : n * 64 + b * 32 + 32, b * 128 : (b + 1) * 128] = (ws[n] * inverse).astype(BF16)
+            log_sum = jnp.where(some, peak + jnp.log2(filled), NEG)
+            for k in range(4):
+                lzs[t * 8 + b * 4 + k] = pltpu.roll(log_sum, 128 - 32 * k, 1) if k else log_sum
+        for d in Z_ORDER:
+            e = (d + NEAR) % NZ
+            if e // 8 == t:
+                remote(lzs.at[e], lz.at[z], l2s, l2r, z_peer(d) * NP + p).start()
+        wait(ro.at[0, pl.ds(0, NP - 1)], r1r.at[t])
+        merged = dot(w_s[t], ro[t].reshape(NREQ, HD), ((0,), (0,)))
+        pzs[t * 8 : (t + 1) * 8] = merged.astype(BF16).reshape(8, 32, HD)
+        if t == 0:
+            for copy in keep:
+                copy.start()
+        for d in Z_ORDER:
+            e = (d + NEAR) % NZ
+            if e // 8 == t:
+                remote(pzs.at[e], pz.at[z], r2s, r2r, z_peer(d) * NP + p).start()
     for copy in keep:
         copy.wait()
 
@@ -307,7 +298,7 @@
         ids = jnp.where(r_group == 0, siv[0][j], siv[1][j])
         own = jnp.sum(jnp.where(r_tok == me * 4 + (r_head >> 3), ids, 0), axis=1, keepdims=True)
         kept = jnp.logical_and(kept, tok_super != own)
-    c_score = dot(qz[z], every_summary, ((1,), (1,))) * SCALE2 + 4.0
+    c_score = dot(qz[NEAR], every_summary, ((1,), (1,))) * SCALE2 + 4.0
     c_score = jnp.where(kept, c_score, NEG)
     c_peak = jnp.max(c_score, axis=1, keepdims=True)
     c_w = jnp.where(kept, jnp.exp2(c_score - c_peak), 0.0)
@@ -327,7 +318,7 @@
     for n in range(NZ):
         result = result + pz[n].astype(F32) * w[:, n : n + 1]
     xs[...] = (result / total).astype(BF16).reshape(NX, 8, HD)
-    keep = pltpu.make_async_copy(xs.at[rep], o_ref.at[rep], loc.at[5])
+    keep = pltpu.make_async_copy(xs.at[rep], o_ref.at[rep], loc.at[8])
     keep.start()
     for d in range(1, NX):
         x = lax.rem(rep + d, NX)
@@ -335,10 +326,12 @@
 
     wait(qz.at[pl.ds(0, NZ - 1)], q1s)
     wait(sz.at[pl.ds(0, NZ - 1)], szs)
-    wait(qs.at[pl.ds(0, NP - 1)], q2s)
+    for t in (0, 1):
+        wait(qs.at[t, pl.ds(0, NP - 1)], q2s)
     wait(sf.at[pl.ds(0, NP - 1)], sfs)
-    wait(os_.at[pl.ds(0, NP - 1)], r1s)
-    wait(ol.at[pl.ds(0, NP - 1)], l1s)
+    for t in (0, 1):
+        wait(os_.at[t, pl.ds(0, NP - 1)], r1s)
+        wait(ol.at[t, pl.ds(0, NP - 1)], l1s)
     wait(pzs.at[pl.ds(0, NZ - 1)], r2s)
     wait(lzs.at[pl.ds(0, NZ - 1)], l2s)
     keep.wait()
@@ -363,17 +356,17 @@
             vmem((SPAN, 2 * HD), BF16),
             vmem((2 * HD, SPAN), BF16),
             vmem((NZ, 32, HD), BF16),
-            vmem((NP, 128, HD), BF16),
-            vmem((NP, 128, HD), BF16),
+            vmem((2, NP, 64, HD), BF16),
+            vmem((2, NP, 64, HD), BF16),
             vmem((NP, NREQ), F32),
-            vmem((NY, 32, 256), F32),
-            vmem((NY, 256, 8), F32),
-            vmem((NP * 128, NREQ), BF16),
-            vmem((NP * 128, NREQ), BF16),
-            vmem((NP, HD, 128), BF16),
-            vmem((NP, 1, 128), F32),
-            vmem((NP, HD, 128), BF16),
-            vmem((NP, 1, 128), F32),
+            vmem((4, 32, 256), F32),
+            vmem((4, 256, 8), F32),
+            vmem((2 * NREQ, 256), BF16),
+            vmem((2, NREQ, 256), BF16),
+            vmem((2, NP, 64, HD), BF16),
+            vmem((2, NP, 1, 128), F32),
+            vmem((2, NP, 64, HD), BF16),
+            vmem((2, NP, 1, 128), F32),
             vmem((NZ, 32, HD), BF16),
             vmem((NZ, 1, 128), F32),
             vmem((NZ, 32, HD), BF16),
@@ -385,12 +378,16 @@
             dma((6,)),
             dma((4,)),
             dma,
+            dma((2,)),
             dma,
+            dma((2, 2)),
             dma,
-            dma((NY,)),
+            dma((2,)),
+            dma,
+            dma((2,)),
         ]
-        + [dma] * 14
-        + [dma((6,))],
+        + [dma] * 10
+        + [dma((9,))],
         compiler_params=pltpu.CompilerParams(collective_id=0, has_side_effects=True),
     )(
         queries.reshape(32, HD),

time: 54.2 us -> 51.3 us (0.946)
  Pallas kernels: 52.7 us -> 49.7 us
    pallas_call x1, Pallas kernels: 52.7 us -> 49.7 us  [shards(): pl.pallas_call(kernel, out_shape=jax.ShapeDtypeStruct((NX, 8, HD), BF16),...]
where the time goes in v4:
time: 51.3 us; the launch traced here: 51 us
  Pallas kernels  49.7 us (97%)
  local copies, waits for them, and re-layouts  1.3 us (3%)
    pallas_call x1, Pallas kernels, shards(): pl.pallas_call(kernel, out_shape=jax.ShapeDtypeStruct((NX, 8, HD), BF16),...  49.7 us
    unnamed x1, local copies, waits for them, and re-layouts  1.3 us

profile of v4, /device:TPU:1, one launch (start us, length us, event | category | flops | bytes accessed | tf_op | source)
XLA Modules:
  0.0 51.0 jit_solution(15252006486664432441)
XLA Ops:
  0.0 49.7 %shard_map.82 = bf16[4,8,128]{2,1,0:T(8,128)(2,1)} custom-call(bf16[32,128]{1,0:T(8,128)(2,1)} %bitcast.10, bf16[2,2048,128]{2,1,0:T(8,128)(2,1)} %kc_h.1, bf16[2,2048,128]{2,1,0:T(8,128)(2,1)} %vc_h.1, bf16[2,128]{1,0:T(2,128)(2,1)} %bitcast.11, bf16[2,128]{1,0:T(2,128)(2,1)} %bitcast.12, s32[1,128]{1,0:T(1,128)} %bitcast.13, s32[2,4,512]{2,1,0:T(4,128)} %bitcast.9, ...), custom_call_target="tpu_custom_call" | custom-call | tf_op jit(solution)/shard_map/pallas_call | solution.py:344
  49.7 1.3 %copy.10 = bf16[1,32,128]{2,1,0:T(8,128)(2,1)} copy(bf16[1,32,128]{2,1,0:T(8,128)(2,1)} %bitcast.8) | data formatting | bytes 16384
